TPU v7x, 32 devices: a whole 2x2x4 slice. The times are simulated.
32 devices in a mesh: section: 2 (over x), expert: 16 (over z, y, core).
Axes of the slice: x: 2, y: 2, z: 4, core: 2. Of those that a mesh axis runs over, the one named last changes fastest.
Arguments:
- images: bfloat16 [32, 256, 1408], P(('section', 'expert')), may hold values from -6 to 6
- norm_gain: bfloat16 [1408], replicated, may hold values from 0.5 to 1.5
- slot_map: bfloat16 [1408, 16], replicated, may hold values from -0.15625 to 0.15625
- logit_scale: float32 [1], replicated, may hold values from 30 to 80
- up_weight: bfloat16 [16, 5120, 1408], P('expert', 'section'), may hold values from -0.625 to 0.625
- down_weight: bfloat16 [16, 5120, 1408], P('expert', 'section'), may hold values from -0.3125 to 0.3125
Outputs:
- block_out: bfloat16 [32, 256, 1408], P(('section', 'expert'))
All inputs are finite; a program needn't handle non-finite values.
Results may differ from a plain program's by a relative error of at most 0.011.
Values may be sent and summed in bfloat16 or wider, within the bound.
A program may use at most 64 MiB of HBM per device.

v0:
```python
import jax
import jax.numpy as jnp
from jax import lax
from jax.sharding import PartitionSpec as P

epsilon = 1e-06


def normalize(inputs, gain_row):
    values = inputs.astype(jnp.float32)
    spread = jnp.mean(values * values, axis=-1, keepdims=True)
    return (values * lax.rsqrt(spread + epsilon) * gain_row.astype(jnp.float32)).astype(
        jnp.bfloat16
    )


def weights_from(raw, normed, slot_cols, scale_now):
    values = normed.astype(jnp.float32)
    token_norm = jnp.sqrt(jnp.sum(values * values, axis=-1) + epsilon)
    columns = slot_cols.astype(jnp.float32)
    column_norm = jnp.sqrt(jnp.sum(columns * columns, axis=0) + epsilon)
    logits = scale_now * raw / (token_norm[:, None, :] * column_norm[None, :, None])
    scores = jnp.exp(logits)
    dispatch = (scores / jnp.sum(scores, axis=-1, keepdims=True)).astype(jnp.bfloat16)
    combine = (scores / jnp.sum(scores, axis=1, keepdims=True)).astype(jnp.bfloat16)
    return (dispatch, combine)


def local(images, norm_gain, slot_map, logit_scale, up_weight, down_weight):
    position = lax.axis_index("section")
    normed = normalize(images, norm_gain)
    raw = jnp.einsum("itd,de->iet", normed, slot_map, preferred_element_type=jnp.float32)
    dispatch, combine = weights_from(raw, normed, slot_map, logit_scale[0])
    slot_in = jnp.einsum(
        "iet,itd->eid", dispatch, normed, preferred_element_type=jnp.float32
    ).astype(jnp.bfloat16)
    slots = lax.all_to_all(slot_in, "expert", split_axis=0, concat_axis=1, tiled=True)
    count = slots.shape[1]
    gathered = lax.all_gather(slots, "section", axis=1, tiled=True)
    hidden = jax.nn.gelu(
        jnp.einsum("esd,efd->esf", gathered, up_weight, preferred_element_type=jnp.float32)
    ).astype(jnp.bfloat16)
    partial_sum = jnp.einsum(
        "esf,efd->esd", hidden, down_weight, preferred_element_type=jnp.float32
    )
    totals = lax.psum(partial_sum, "section")
    own_rows = lax.dynamic_slice_in_dim(totals, position * count, count, 1)
    result = own_rows.astype(jnp.bfloat16)
    back = lax.all_to_all(result, "expert", split_axis=1, concat_axis=0, tiled=True)
    mixed = jnp.einsum("iet,eid->itd", combine, back, preferred_element_type=jnp.float32)
    return (images.astype(jnp.float32) + mixed).astype(jnp.bfloat16)


def solution(mesh):
    return jax.shard_map(
        local,
        mesh=mesh,
        in_specs=(
            P(("section", "expert"), None, None),
            P(),
            P(),
            P(),
            P("expert", "section", None),
            P("expert", "section", None),
        ),
        out_specs=P(("section", "expert"), None, None),
        check_vma=False,
    )
```

profile of v0, /device:TPU:0, one launch (start us, length us, event | category | flops | bytes accessed | tf_op | source)
XLA Modules:
  0.0 58.3 jit_solution(4352403339752684257)
XLA Ops:
  0.0 0.0 copy-start.1
  0.7 0.9 %multiply_reduce_fusion.1 = f32[16]{0:T(128)S(1)} fusion(bf16[1408,16]{0,1:T(8,128)(2,1)} %param.8), kind=kLoop, calls=%fused_computation.37 | loop fusion | flops 67568 | bytes 45120 | tf_op jit(solution)/shard_map/reduce_sum | solution.py:21
  1.6 1.3 %fusion.10 = f32[256]{0:T(256)S(1)} fusion(bf16[1,256,1408]{2,1,0:T(8,128)(2,1)} %param.6), kind=kLoop, calls=%fused_computation.12 | loop fusion | flops 1081088 | bytes 721920 | tf_op jit(solution)/shard_map/reduce_sum | solution.py:11
  3.0 0.7 %convert_element_type.44 = f32[1408]{0:T(1024)S(1)} convert(bf16[1408]{0:T(1024)(128)(2,1)} %param.7) | non-fusion elementwise | flops 1408 | bytes 8448 | tf_op jit(solution)/shard_map/convert_element_type | solution.py:12
  3.7 1.5 %multiply_reduce_fusion = f32[256]{0:T(256)S(1)} fusion(f32[1408]{0:T(1024)S(1)} %convert_element_type.44, f32[256]{0:T(256)S(1)} %add_rsqrt_fusion, bf16[1,256,1408]{2,1,0:T(8,128)(2,1)} %param.6), kind=kLoop, calls=%fused_computation.15 | loop fusion | flops 2522880 | bytes 728576 | tf_op jit(solution)/shard_map/reduce_sum | solution.py:19
  5.2 0.0 copy-done.1
  5.2 0.0 copy-done
  5.2 0.5 fusion.48
  5.7 0.4 fusion.9
  6.1 0.6 %broadcast.46 = bf16[]{:T(256)} broadcast(bf16[]{:T(256)} %constant.65), dimensions={} | broadcast | bytes 4 | tf_op jit(solution)/shard_map/convert_element_type | solution.py:36
  6.7 0.7 %reduce.6 = bf16[16,1408]{1,0:T(8,128)(2,1)S(1)} reduce(bf16[16,1,1408]{2,0,1:T(8,128)(2,1)S(1)} %fusion.9, bf16[]{:T(256)} %broadcast.46), dimensions={1}, to_apply=%copy.9.reduce_sub_computation | reduce | bytes 90114 | tf_op jit(solution)/shard_map/convert_element_type | solution.py:36
  7.4 0.7 %reshape.104 = bf16[16,2,704]{2,1,0:T(2,128)(2,1)} reshape(bf16[16,1408]{1,0:T(8,128)(2,1)S(1)} %reduce.6) | data formatting | bytes 90112
  8.1 7.4 %all-to-all-start = ((bf16[16,2,704]{2,1,0:T(2,128)(2,1)}), bf16[16,2,704]{2,1,0:T(2,128)(2,1)S(1)}, u32[]{:S(2)}, u32[]{:S(2)}) async-start(bf16[16,2,704]{2,1,0:T(2,128)(2,1)} %reshape.104), calls=%async_computation | async-start | bytes 98304 | tf_op jit(solution)/shard_map/all_to_all | solution.py:37
  15.5 6.8 %all-to-all-done = bf16[16,2,704]{2,1,0:T(2,128)(2,1)S(1)} async-done(((bf16[16,2,704]{2,1,0:T(2,128)(2,1)}), bf16[16,2,704]{2,1,0:T(2,128)(2,1)S(1)}, u32[]{:S(2)}, u32[]{:S(2)}) %all-to-all-start) | async-done | bytes 45088 | tf_op jit(solution)/shard_map/all_to_all | solution.py:37
  22.3 0.1 reshape.105
  22.4 4.7 %all-gather = bf16[32,1,1408]{2,0,1:T(8,128)(2,1)S(1)} all-gather(bf16[16,1,1408]{2,0,1:T(8,128)(2,1)S(1)} %copy.10), channel_id=2, replica_groups=mesh['section'=2,'expert'=16] {'section'}, dimensions={0}, use_global_device_ids=true | all-gather | bytes 135168 | tf_op jit(solution)/shard_map/all_gather | solution.py:39
  27.2 8.4 %fusion.6 = f32[1,32,1408]{2,1,0:T(8,128)S(1)} fusion(bf16[1,2560,1408]{2,1,0:T(8,128)(2,1)} %param.11, bf16[1,2560,1408]{2,1,0:T(8,128)(2,1)} %param.10, bf16[32,1,1408]{2,0,1:T(8,128)(2,1)S(1)} %all-gather), kind=kOutput, calls=%fused_computation.7 | convolution fusion | flops 462110720 | bytes 14688256 | tf_op jit(solution)/shard_map/esf,efd->esd/dot_general | solution.py:43
  35.6 10.9 %all-reduce.1 = bf16[1,32,1408]{2,1,0:T(8,128)(2,1)S(1)} all-reduce(f32[1,32,1408]{2,1,0:T(8,128)S(1)} %fusion.6), channel_id=1, replica_groups=mesh['section'=2,'expert'=16] {'section'}, use_global_device_ids=true, to_apply=%region_5.0 | all-reduce | flops 45056 | bytes 270336 | tf_op jit(solution)/shard_map/psum | solution.py:46
  46.5 0.1 copy.18
  46.6 0.9 %reduce.7 = bf16[16,1408]{1,0:T(8,128)(2,1)S(1)} reduce(bf16[16,1,1408]{2,1,0:T(2,128)(2,1)S(1)} %bitcast.53, bf16[]{:T(256)} %broadcast.46), dimensions={1}, to_apply=%bitcast.51.reduce_sub_computation | reduce | bytes 90114
  47.5 0.1 reshape.106
  47.6 9.3 %all_to_all.21 = bf16[16,2,704]{2,1,0:T(2,128)(2,1)S(1)} all-to-all(bf16[16,2,704]{2,1,0:T(2,128)(2,1)S(1)} %reshape.106), channel_id=1, replica_groups=mesh['section'=2,'expert'=16] {'expert'}, dimensions={0} | all-to-all | bytes 90112 | tf_op jit(solution)/shard_map/all_to_all | solution.py:49
  57.0 0.1 reshape.107
  57.1 1.3 %fusion.5 = bf16[1,256,1408]{2,1,0:T(8,128)(2,1)} fusion(bf16[1,256,1408]{2,1,0:T(8,128)(2,1)S(1)} %copy-done, bf16[1,16,1408]{2,0,1:T(2,128)(2,1)S(1)} %bitcast.54, f32[16,256]{1,0:T(8,128)S(1)} %get-tuple-element.7, f32[256]{0:T(256)S(1)} %get-tuple-element.5), kind=kOutput, calls=%fused_computation.6 | convolution fusion | flops 12623872 | bytes 1504256 | tf_op jit(solution)/shard_map/iet,eid->itd/dot_general | solution.py:50
  (6 shorter events, 0.1 us)
Async XLA Ops:
  0.0 5.2 %copy-start.1 = (bf16[1408,16]{0,1:T(8,128)(2,1)S(1)}, bf16[1408,16]{0,1:T(8,128)(2,1)}, u32[]{:S(2)}) copy-start(bf16[1408,16]{0,1:T(8,128)(2,1)} %param.8) | copy-start | bytes 135172
  0.0 5.2 %copy-start = (bf16[1,256,1408]{2,1,0:T(8,128)(2,1)S(1)}, bf16[1,256,1408]{2,1,0:T(8,128)(2,1)}, u32[]{:S(2)}) copy-start(bf16[1,256,1408]{2,1,0:T(8,128)(2,1)} %param.6) | copy-start | bytes 2162692
  8.1 14.2 %all-to-all-start = ((bf16[16,2,704]{2,1,0:T(2,128)(2,1)}), bf16[16,2,704]{2,1,0:T(2,128)(2,1)S(1)}, u32[]{:S(2)}, u32[]{:S(2)}) async-start(bf16[16,2,704]{2,1,0:T(2,128)(2,1)} %reshape.104), calls=%async_computation | async-start | bytes 98304 | tf_op jit(solution)/shard_map/all_to_all | solution.py:37
where the time goes:
time: 58.8 us; the launch traced here: 58.3 us
  blocking collectives  24.9 us (42%)
  matrix products  10.6 us (18%)
  starting transfers between devices  7.41 us (13%)
  waiting for transfers between devices  6.76 us (11%)
  other arithmetic  6.08 us (10%)
  local copies, waits for them, and re-layouts  1.79 us (3%)
  between operations  0.82 us (1%)
    psum x1, blocking collectives, local(): totals = lax.psum(partial_sum, 'section')  10.9 us
    all_to_all x1, blocking collectives, local(): lax.all_to_all(result, 'expert', split_axis=1, concat_axis=0, tiled=True)  9.34 us
    dot_general x1, matrix products, local(): jnp.einsum('esf,efd->esd', hidden, down_weight, preferred_element_type=jn...  8.44 us
    all_to_all x1, starting transfers between devices, local(): lax.all_to_all(slot_in, 'expert', split_axis=0, concat_axis=1, tiled=True)  7.41 us
    all_to_all x1, waiting for transfers between devices, local(): lax.all_to_all(slot_in, 'expert', split_axis=0, concat_axis=1, tiled=True)  6.76 us
    all_gather x1, blocking collectives, local(): gathered = lax.all_gather(slots, 'section', axis=1, tiled=True)  4.71 us
    reduce_sum x1, other arithmetic, weights_from(): token_norm = jnp.sqrt(jnp.sum(values * values, axis=-1) + epsilon)  1.48 us
    reduce_sum x1, other arithmetic, normalize(): spread = jnp.mean(values * values, axis=-1, keepdims=True)  1.34 us
  transfers between devices with their start and end apart: 1, of which 1 were waited for; matrix products, arithmetic and copies ran while one was open for 0% of the time, Pallas kernels for 0%

commit v1 on v0

--- a/solution.py
+++ b/solution.py
@@ -43,7 +43,7 @@
     partial_sum = jnp.einsum(
         "esf,efd->esd", hidden, down_weight, preferred_element_type=jnp.float32
     )
-    totals = lax.psum(partial_sum, "section")
+    totals = jnp.sum(lax.all_gather(partial_sum, "section"), axis=0)
     own_rows = lax.dynamic_slice_in_dim(totals, position * count, count, 1)
     result = own_rows.astype(jnp.bfloat16)
     back = lax.all_to_all(result, "expert", split_axis=1, concat_axis=0, tiled=True)

time: 58.8 us -> 54.1 us (0.920)
  blocking collectives: 24.9 us -> 20.2 us
    psum x1 -> x0, blocking collectives: 10.9 us -> none  [local(): totals = lax.psum(partial_sum, 'section')]
    all_gather x0 -> x1, blocking collectives: none -> 6.17 us  [local(): totals = jnp.sum(lax.all_gather(partial_sum, 'section'), axis=0)]
where the time goes in v1:
time: 54.1 us; the launch traced here: 53.7 us
  blocking collectives  20.2 us (37%)
  matrix products  10.6 us (20%)
  starting transfers between devices  7.41 us (14%)
  waiting for transfers between devices  6.76 us (12%)
  other arithmetic  6.1 us (11%)
  local copies, waits for them, and re-layouts  1.79 us (3%)
  between operations  0.81 us (1%)
    all_to_all x1, blocking collectives, local(): lax.all_to_all(result, 'expert', split_axis=1, concat_axis=0, tiled=True)  9.34 us
    dot_general x1, matrix products, local(): jnp.einsum('esf,efd->esd', hidden, down_weight, preferred_element_type=jn...  8.44 us
    all_to_all x1, starting transfers between devices, local(): lax.all_to_all(slot_in, 'expert', split_axis=0, concat_axis=1, tiled=True)  7.41 us
    all_to_all x1, waiting for transfers between devices, local(): lax.all_to_all(slot_in, 'expert', split_axis=0, concat_axis=1, tiled=True)  6.76 us
    all_gather x1, blocking collectives, local(): totals = jnp.sum(lax.all_gather(partial_sum, 'section'), axis=0)  6.17 us
    all_gather x1, blocking collectives, local(): gathered = lax.all_gather(slots, 'section', axis=1, tiled=True)  4.71 us
    reduce_sum x1, other arithmetic, weights_from(): token_norm = jnp.sqrt(jnp.sum(values * values, axis=-1) + epsilon)  1.48 us
    reduce_sum x1, other arithmetic, normalize(): spread = jnp.mean(values * values, axis=-1, keepdims=True)  1.34 us
  transfers between devices with their start and end apart: 1, of which 1 were waited for; matrix products, arithmetic and copies ran while one was open for 0% of the time, Pallas kernels for 0%

profile of v1, /device:TPU:0, one launch (start us, length us, event | category | flops | bytes accessed | tf_op | source)
XLA Modules:
  0.0 53.7 jit_solution(17233985536007423341)
XLA Ops:
  0.0 0.0 copy-start.1
  0.7 0.9 %multiply_reduce_fusion.1 = f32[16]{0:T(128)S(1)} fusion(bf16[1408,16]{0,1:T(8,128)(2,1)} %param.8), kind=kLoop, calls=%fused_computation.36 | loop fusion | flops 67568 | bytes 45120 | tf_op jit(solution)/shard_map/reduce_sum | solution.py:21
  1.6 1.3 %fusion.7 = f32[256]{0:T(256)S(1)} fusion(bf16[1,256,1408]{2,1,0:T(8,128)(2,1)} %param.6), kind=kLoop, calls=%fused_computation.11 | loop fusion | flops 1081088 | bytes 721920 | tf_op jit(solution)/shard_map/reduce_sum | solution.py:11
  3.0 0.7 %convert_element_type.47 = f32[1408]{0:T(1024)S(1)} convert(bf16[1408]{0:T(1024)(128)(2,1)} %param.7) | non-fusion elementwise | flops 1408 | bytes 8448 | tf_op jit(solution)/shard_map/convert_element_type | solution.py:12
  3.7 1.5 %multiply_reduce_fusion = f32[256]{0:T(256)S(1)} fusion(f32[1408]{0:T(1024)S(1)} %convert_element_type.47, f32[256]{0:T(256)S(1)} %add_rsqrt_fusion, bf16[1,256,1408]{2,1,0:T(8,128)(2,1)} %param.6), kind=kLoop, calls=%fused_computation.14 | loop fusion | flops 2522880 | bytes 728576 | tf_op jit(solution)/shard_map/reduce_sum | solution.py:19
  5.2 0.0 copy-done.1
  5.2 0.0 copy-done
  5.2 0.5 fusion.46
  5.7 0.4 fusion.6
  6.1 0.6 %broadcast.46 = bf16[]{:T(256)} broadcast(bf16[]{:T(256)} %constant.65), dimensions={} | broadcast | bytes 4 | tf_op jit(solution)/shard_map/convert_element_type | solution.py:36
  6.7 0.7 %reduce.8 = bf16[16,1408]{1,0:T(8,128)(2,1)S(1)} reduce(bf16[16,1,1408]{2,0,1:T(8,128)(2,1)S(1)} %fusion.6, bf16[]{:T(256)} %broadcast.46), dimensions={1}, to_apply=%copy.8.reduce_sub_computation | reduce | bytes 90114 | tf_op jit(solution)/shard_map/convert_element_type | solution.py:36
  7.4 0.7 %reshape.110 = bf16[16,2,704]{2,1,0:T(2,128)(2,1)} reshape(bf16[16,1408]{1,0:T(8,128)(2,1)S(1)} %reduce.8) | data formatting | bytes 90112
  8.1 7.4 %all-to-all-start = ((bf16[16,2,704]{2,1,0:T(2,128)(2,1)}), bf16[16,2,704]{2,1,0:T(2,128)(2,1)S(1)}, u32[]{:S(2)}, u32[]{:S(2)}) async-start(bf16[16,2,704]{2,1,0:T(2,128)(2,1)} %reshape.110), calls=%async_computation | async-start | bytes 98304 | tf_op jit(solution)/shard_map/all_to_all | solution.py:37
  15.5 6.8 %all-to-all-done = bf16[16,2,704]{2,1,0:T(2,128)(2,1)S(1)} async-done(((bf16[16,2,704]{2,1,0:T(2,128)(2,1)}), bf16[16,2,704]{2,1,0:T(2,128)(2,1)S(1)}, u32[]{:S(2)}, u32[]{:S(2)}) %all-to-all-start) | async-done | bytes 45088 | tf_op jit(solution)/shard_map/all_to_all | solution.py:37
  22.3 0.1 reshape.111
  22.4 4.7 %all-gather = bf16[32,1,1408]{2,0,1:T(8,128)(2,1)S(1)} all-gather(bf16[16,1,1408]{2,0,1:T(8,128)(2,1)S(1)} %copy.9), channel_id=2, replica_groups=mesh['section'=2,'expert'=16] {'section'}, dimensions={0}, use_global_device_ids=true | all-gather | bytes 135168 | tf_op jit(solution)/shard_map/all_gather | solution.py:39
  27.2 8.4 %fusion = f32[32,1408]{1,0:T(8,128)S(1)} fusion(bf16[1,2560,1408]{2,1,0:T(8,128)(2,1)} %param.11, bf16[1,2560,1408]{2,1,0:T(8,128)(2,1)} %param.10, bf16[32,1,1408]{2,0,1:T(8,128)(2,1)S(1)} %all-gather), kind=kOutput, calls=%fused_computation | convolution fusion | flops 462110720 | bytes 14688256 | tf_op jit(solution)/shard_map/esf,efd->esd/dot_general | solution.py:43
  35.6 6.2 %all-gather.1 = f32[64,1408]{1,0:T(8,128)S(1)} all-gather(f32[32,1408]{1,0:T(8,128)S(1)} %fusion), channel_id=3, replica_groups=mesh['section'=2,'expert'=16] {'section'}, dimensions={0}, use_global_device_ids=true | all-gather | bytes 540672 | tf_op jit(solution)/shard_map/all_gather | solution.py:46
  41.8 0.1 copy.17
  41.9 0.9 %reduce.9 = bf16[16,1408]{1,0:T(8,128)(2,1)S(1)} reduce(bf16[16,1,1408]{2,1,0:T(2,128)(2,1)S(1)} %bitcast.53, bf16[]{:T(256)} %broadcast.46), dimensions={1}, to_apply=%bitcast.50.reduce_sub_computation | reduce | bytes 90114
  42.8 0.1 reshape.112
  42.9 9.3 %all_to_all.21 = bf16[16,2,704]{2,1,0:T(2,128)(2,1)S(1)} all-to-all(bf16[16,2,704]{2,1,0:T(2,128)(2,1)S(1)} %reshape.112), channel_id=1, replica_groups=mesh['section'=2,'expert'=16] {'expert'}, dimensions={0} | all-to-all | bytes 90112 | tf_op jit(solution)/shard_map/all_to_all | solution.py:49
  52.3 0.1 reshape.113
  52.4 1.3 %fusion.5 = bf16[1,256,1408]{2,1,0:T(8,128)(2,1)} fusion(bf16[1,256,1408]{2,1,0:T(8,128)(2,1)S(1)} %copy-done, bf16[1,16,1408]{2,0,1:T(2,128)(2,1)S(1)} %bitcast.54, f32[16,256]{1,0:T(8,128)S(1)} %get-tuple-element.7, f32[256]{0:T(256)S(1)} %get-tuple-element.5), kind=kOutput, calls=%fused_computation.6 | convolution fusion | flops 12623872 | bytes 1504256 | tf_op jit(solution)/shard_map/iet,eid->itd/dot_general | solution.py:50
  (7 shorter events, 0.1 us)
Async XLA Ops:
  0.0 5.2 %copy-start.1 = (bf16[1408,16]{0,1:T(8,128)(2,1)S(1)}, bf16[1408,16]{0,1:T(8,128)(2,1)}, u32[]{:S(2)}) copy-start(bf16[1408,16]{0,1:T(8,128)(2,1)} %param.8) | copy-start | bytes 135172
  0.0 5.2 %copy-start = (bf16[1,256,1408]{2,1,0:T(8,128)(2,1)S(1)}, bf16[1,256,1408]{2,1,0:T(8,128)(2,1)}, u32[]{:S(2)}) copy-start(bf16[1,256,1408]{2,1,0:T(8,128)(2,1)} %param.6) | copy-start | bytes 2162692
  8.1 14.2 %all-to-all-start = ((bf16[16,2,704]{2,1,0:T(2,128)(2,1)}), bf16[16,2,704]{2,1,0:T(2,128)(2,1)S(1)}, u32[]{:S(2)}, u32[]{:S(2)}) async-start(bf16[16,2,704]{2,1,0:T(2,128)(2,1)} %reshape.110), calls=%async_computation | async-start | bytes 98304 | tf_op jit(solution)/shard_map/all_to_all | solution.py:37
